TPU v7x, 256 devices: a whole 4x4x8 slice. The times are simulated.
256 devices in a mesh: clip: 32 (over y_lo, z, core), row: 8 (over x, y_hi).
Axes of the slice: x: 4, y: 4 (y_hi: 2, y_lo: 2; y = y_hi * 2 + y_lo), z: 8, core: 2. Of those that a mesh axis runs over, the one named last changes fastest.
Arguments:
- video: bfloat16 [128, 64, 320, 128], P('clip', 'row'), may hold values from -6 to 6
- spatial_one: bfloat16 [3, 3, 320, 320], replicated, may hold values from -0.109375 to 0.109375
- spatial_two: bfloat16 [3, 3, 320, 320], replicated, may hold values from -0.109375 to 0.109375
- temporal_mix: bfloat16 [3, 320, 320], replicated, may hold values from -0.1875 to 0.1875
- bias_one: float32 [320], replicated, may hold values from -3 to 3
- bias_two: float32 [320], replicated, may hold values from -3 to 3
- bias_three: float32 [320], replicated, may hold values from -3 to 3
Outputs:
- block_out: bfloat16 [128, 64, 320, 128], P('clip', 'row')
All inputs are finite; a program needn't handle non-finite values.
Results may differ from a plain program's by a relative error of at most 0.011.
Values may be sent and summed in bfloat16 or wider, within the bound.
No kernel may reach another device: no remote copies, remote signals or barrier semaphores. Data moves between devices by JAX's collectives and lax.ppermute only.
A program may use at most 128 MiB of HBM per device.

v0:
```python
import jax
import jax.numpy as jnp
from jax import lax
from jax.sharding import PartitionSpec as P


def padded(x, sides, width):
    for axis, dim in sides:
        size, length = (lax.axis_size(axis), x.shape[dim])
        up = [(i, (i + 1) % size) for i in range(size - 1)]
        down = [(j, i) for i, j in up]
        last = lax.slice_in_dim(x, length - width, length, axis=dim)
        first = lax.slice_in_dim(x, 0, width, axis=dim)
        before = lax.ppermute(last, axis, up)
        after = lax.ppermute(first, axis, down)
        x = jnp.concatenate([before, x, after], axis=dim)
    return x


def silu_round(values):
    return jax.nn.silu(values.astype(jnp.float32)).astype(jnp.bfloat16)


def conv_rows(activated, kernel):
    row_count = activated.shape[1] - 2
    partials = []
    for column_tap in range(3):
        partial_value = None
        for row_tap in range(3):
            product = jnp.einsum(
                "oc,frcw->frow",
                kernel[row_tap, column_tap],
                activated[:, row_tap : row_tap + row_count],
                preferred_element_type=jnp.float32,
            )
            partial_value = product if partial_value is None else partial_value + product
        partials.append(partial_value)
    zero_col = jnp.zeros(partials[0].shape[:-1] + (1,), jnp.float32)
    shifted_in = jnp.concatenate([zero_col, partials[0][..., :-1]], axis=3)
    shifted_out = jnp.concatenate([partials[2][..., 1:], zero_col], axis=3)
    return shifted_in + partials[1] + shifted_out


def residual_add(residual_in, bias_vec, convolved):
    return (residual_in.astype(jnp.float32) + bias_vec[:, None] + convolved).astype(jnp.bfloat16)


def spatial_chain(frames, spatial_one, spatial_two, bias_one, bias_two):

    def rimmed(activated):
        return padded(activated, (("row", 1),), 1)

    first_out = residual_add(frames, bias_one, conv_rows(rimmed(silu_round(frames)), spatial_one))
    second = residual_add(
        first_out, bias_two, conv_rows(rimmed(silu_round(first_out)), spatial_two)
    )
    return second


def body(video, spatial_one, spatial_two, temporal_mix, bias_one, bias_two, bias_three):
    frame_count = video.shape[0]
    centre = spatial_chain(video, spatial_one, spatial_two, bias_one, bias_two)
    activated = padded(silu_round(centre), (("clip", 0),), 1)
    mixed_out = centre.astype(jnp.float32) + bias_three[:, None]
    for frame_tap in range(3):
        mixed_out = mixed_out + jnp.einsum(
            "oc,frcw->frow",
            temporal_mix[frame_tap],
            activated[frame_tap : frame_tap + frame_count],
            preferred_element_type=jnp.float32,
        )
    return mixed_out.astype(jnp.bfloat16)


def solution(mesh):
    placed = (P("clip", "row", None, None), P(), P(), P(), P(), P(), P())
    return jax.shard_map(
        body, mesh=mesh, in_specs=placed, out_specs=P("clip", "row", None, None), check_vma=False
    )
```

profile of v0, /device:TPU:113, one launch (start us, length us, event | category | flops | bytes accessed | tf_op | source)
XLA Modules:
  0.0 111.8 jit_solution(1849481339109321292)
XLA Ops:
  0.0 3.2 %fusion.5 = bf16[4,8,320,128]{3,2,1,0:T(8,128)(2,1)S(1)} fusion(bf16[4,8,320,128]{3,2,1,0:T(8,128)(2,1)} %param.7), kind=kLoop, calls=%fused_computation.14 | loop fusion | flops 7864320 | bytes 5242880 | tf_op jit(solution)/shard_map/convert_element_type | solution.py:21
  3.3 2.0 %collective-permute-start.1 = (bf16[4,1,320,128]{3,2,1,0:T(8,128)(2,1)S(1)}, bf16[4,1,320,128]{3,2,1,0:T(8,128)(2,1)S(1)}, u32[]{:S(2)}, u32[]{:S(2)}) collective-permute-start(bf16[4,1,320,128]{3,2,1,0:T(8,128)(2,1)S(1)} %get-tuple-element.9), channel_id=1, source_target_pairs={{1,0},{2,1},{3,2},{4,3},{5,4},{6,5},{7,6},{9,8},{10,9},{11,10},{12... | collective-permute-start | bytes 983048 | tf_op jit(solution)/shard_map/ppermute | solution.py:15
  5.3 5.7 %collective-permute-start = (bf16[4,1,320,128]{3,2,1,0:T(8,128)(2,1)S(1)}, bf16[4,1,320,128]{3,2,1,0:T(8,128)(2,1)S(1)}, u32[]{:S(2)}, u32[]{:S(2)}) collective-permute-start(bf16[4,1,320,128]{3,2,1,0:T(8,128)(2,1)S(1)} %get-tuple-element.10), channel_id=1, source_target_pairs={{0,1},{1,2},{2,3},{3,4},{4,5},{5,6},{6,7},{8,9},{9,10},{10,11},{11... | collective-permute-start | bytes 983048 | tf_op jit(solution)/shard_map/ppermute | solution.py:14
  15.6 8.7 %collective-permute-done = bf16[4,1,320,128]{3,2,1,0:T(8,128)(2,1)S(1)} collective-permute-done((bf16[4,1,320,128]{3,2,1,0:T(8,128)(2,1)S(1)}, bf16[4,1,320,128]{3,2,1,0:T(8,128)(2,1)S(1)}, u32[]{:S(2)}, u32[]{:S(2)}) %collective-permute-start) | collective-permute-done | bytes 327712 | tf_op jit(solution)/shard_map/ppermute | solution.py:14
  25.8 1.6 %add_bitcast_fusion.2 = f32[4,8,320,128]{3,2,1,0:T(8,128)S(1)} fusion(f32[4,8,128,320]{2,3,1,0:T(8,128)S(1)} %fusion.27, f32[4,8,128,320]{2,3,1,0:T(8,128)S(1)} %fusion.55, bf16[4,1,320,128]{3,2,1,0:T(8,128)(2,1)S(1)} %collective-permute-done.1, bf16[4,8,320,128]{3,2,1,0:T(8,128)(2,1)S(1)} %fusion.5, bf16[3,3,320,320]{3,2,1,0:T(8,128)(2,1)S(1)} %copy-done.1), kind=kOutput, calls=%fused_computation.35 | convolution fusion | flops 846725120 | bytes 18923520 | tf_op jit(solution)/shard_map/oc,frcw->frow/dot_general | solution.py:30
  28.8 2.5 %fusion.26 = f32[4,8,128,320]{2,3,1,0:T(8,128)S(1)} fusion(bf16[4,8,320,128]{3,2,1,0:T(8,128)(2,1)S(1)} %fusion.5, bf16[4,1,320,128]{3,2,1,0:T(8,128)(2,1)S(1)} %collective-permute-done, bf16[3,3,320,320]{3,2,1,0:T(8,128)(2,1)} %param.8), kind=kOutput, calls=%fused_computation.47 | convolution fusion | flops 844103680 | bytes 8437760 | tf_op jit(solution)/shard_map/oc,frcw->frow/dot_general | solution.py:30
  31.3 2.5 %fusion.28 = f32[4,8,128,320]{2,3,1,0:T(8,128)S(1)} fusion(bf16[4,8,320,128]{3,2,1,0:T(8,128)(2,1)S(1)} %fusion.5, bf16[4,1,320,128]{3,2,1,0:T(8,128)(2,1)S(1)} %collective-permute-done, bf16[3,3,320,320]{3,2,1,0:T(8,128)(2,1)} %param.8), kind=kOutput, calls=%fused_computation.49 | convolution fusion | flops 844103680 | bytes 8437760 | tf_op jit(solution)/shard_map/oc,frcw->frow/dot_general | solution.py:30
  33.9 4.9 %add_bitcast_fusion.3 = f32[4,8,320,128]{3,2,1,0:T(8,128)} fusion(f32[4,8,128,320]{2,3,1,0:T(8,128)S(1)} %fusion.28, f32[4,8,128,320]{2,3,1,0:T(8,128)S(1)} %fusion.63, bf16[4,1,320,128]{3,2,1,0:T(8,128)(2,1)S(1)} %collective-permute-done.1, bf16[4,8,320,128]{3,2,1,0:T(8,128)(2,1)S(1)} %fusion.5, bf16[3,3,320,320]{3,2,1,0:T(8,128)(2,1)} %param.8), kind=kOutput, calls=%fused_computation.36 | convolution fusion | flops 846725120 | bytes 18923520 | tf_op jit(solution)/shard_map/oc,frcw->frow/dot_general | solution.py:30
  38.8 7.3 %fusion.11 = (bf16[4,8,320,128]{3,2,1,0:T(8,128)(2,1)S(1)}, bf16[4,8,320,128]{3,2,1,0:T(8,128)(2,1)}) fusion(f32[4,8,320,127]{3,2,1,0:T(8,128)S(1)} %slice.165, bf16[4,1,320,128]{3,2,1,0:T(8,128)(2,1)} %copy-done.4, bf16[4,8,320,128]{3,2,1,0:T(8,128)(2,1)S(1)} %fusion.5, bf16[3,3,320,320]{3,2,1,0:T(8,128)(2,1)} %param.8, ...), kind=kOutput, calls=%fused_computation.20 | convolution fusion | flops 862453760 | bytes 31991040 | tf_op jit(solution)/shard_map/oc,frcw->frow/dot_general | solution.py:30
  46.1 2.6 %fusion.51 = f32[4,8,128,320]{2,3,1,0:T(8,128)S(1)} fusion(bf16[4,8,320,128]{3,2,1,0:T(8,128)(2,1)S(1)} %get-tuple-element.11, bf16[3,3,320,320]{3,2,1,0:T(8,128)(2,1)} %param.9), kind=kOutput, calls=%fused_computation.72 | convolution fusion | flops 838860800 | bytes 8110080 | tf_op jit(solution)/shard_map/oc,frcw->frow/dot_general | solution.py:30
  50.3 1.9 %collective-permute-start.3 = (bf16[4,1,320,128]{3,2,1,0:T(8,128)(2,1)S(1)}, bf16[4,1,320,128]{3,2,1,0:T(8,128)(2,1)S(1)}, u32[]{:S(2)}, u32[]{:S(2)}) collective-permute-start(bf16[4,1,320,128]{3,2,1,0:T(8,128)(2,1)S(1)} %get-tuple-element.7), channel_id=1, source_target_pairs={{1,0},{2,1},{3,2},{4,3},{5,4},{6,5},{7,6},{9,8},{10,9},{11,10},{12... | collective-permute-start | bytes 983048 | tf_op jit(solution)/shard_map/ppermute | solution.py:15
  52.2 5.8 %collective-permute-start.2 = (bf16[4,1,320,128]{3,2,1,0:T(8,128)(2,1)S(1)}, bf16[4,1,320,128]{3,2,1,0:T(8,128)(2,1)S(1)}, u32[]{:S(2)}, u32[]{:S(2)}) collective-permute-start(bf16[4,1,320,128]{3,2,1,0:T(8,128)(2,1)S(1)} %get-tuple-element.8), channel_id=1, source_target_pairs={{0,1},{1,2},{2,3},{3,4},{4,5},{5,6},{6,7},{8,9},{9,10},{10,11},{11... | collective-permute-start | bytes 983048 | tf_op jit(solution)/shard_map/ppermute | solution.py:14
  59.5 11.7 %collective-permute-done.2 = bf16[4,1,320,128]{3,2,1,0:T(8,128)(2,1)S(1)} collective-permute-done((bf16[4,1,320,128]{3,2,1,0:T(8,128)(2,1)S(1)}, bf16[4,1,320,128]{3,2,1,0:T(8,128)(2,1)S(1)}, u32[]{:S(2)}, u32[]{:S(2)}) %collective-permute-start.2) | collective-permute-done | bytes 327712 | tf_op jit(solution)/shard_map/ppermute | solution.py:14
  71.2 1.5 %fusion.33 = f32[4,8,128,320]{2,3,1,0:T(8,128)S(1)} fusion(bf16[4,8,320,128]{3,2,1,0:T(8,128)(2,1)S(1)} %get-tuple-element.11, bf16[4,1,320,128]{3,2,1,0:T(8,128)(2,1)S(1)} %collective-permute-done.2, bf16[3,3,320,320]{3,2,1,0:T(8,128)(2,1)S(1)} %copy-done.2), kind=kOutput, calls=%fused_computation.54 | convolution fusion | flops 844103680 | bytes 8437760 | tf_op jit(solution)/shard_map/oc,frcw->frow/dot_general | solution.py:30
  72.8 1.8 %add_bitcast_fusion = f32[4,8,320,128]{3,2,1,0:T(8,128)S(1)} fusion(f32[4,8,128,320]{2,3,1,0:T(8,128)S(1)} %fusion.33, f32[4,8,128,320]{2,3,1,0:T(8,128)S(1)} %fusion.43, bf16[4,1,320,128]{3,2,1,0:T(8,128)(2,1)S(1)} %collective-permute-done.3, bf16[4,8,320,128]{3,2,1,0:T(8,128)(2,1)S(1)} %get-tuple-element.11, bf16[3,3,320,320]{3,2,1,0:T(8,128)(2,1)S(1)} %copy-done.2), kind=kOutput, calls=%fused_computation.33 | convolution fusion | flops 846725120 | bytes 18923520 | tf_op jit(solution)/shard_map/oc,frcw->frow/dot_general | solution.py:30
  76.0 1.5 %fusion.32 = f32[4,8,128,320]{2,3,1,0:T(8,128)S(1)} fusion(bf16[4,8,320,128]{3,2,1,0:T(8,128)(2,1)S(1)} %get-tuple-element.11, bf16[4,1,320,128]{3,2,1,0:T(8,128)(2,1)S(1)} %collective-permute-done.2, bf16[3,3,320,320]{3,2,1,0:T(8,128)(2,1)S(1)} %copy-done.2), kind=kOutput, calls=%fused_computation.53 | convolution fusion | flops 844103680 | bytes 8437760 | tf_op jit(solution)/shard_map/oc,frcw->frow/dot_general | solution.py:30
  77.5 1.5 %fusion.34 = f32[4,8,128,320]{2,3,1,0:T(8,128)S(1)} fusion(bf16[4,8,320,128]{3,2,1,0:T(8,128)(2,1)S(1)} %get-tuple-element.11, bf16[4,1,320,128]{3,2,1,0:T(8,128)(2,1)S(1)} %collective-permute-done.2, bf16[3,3,320,320]{3,2,1,0:T(8,128)(2,1)S(1)} %copy-done.2), kind=kOutput, calls=%fused_computation.55 | convolution fusion | flops 844103680 | bytes 8437760 | tf_op jit(solution)/shard_map/oc,frcw->frow/dot_general | solution.py:30
  79.1 3.9 %add_bitcast_fusion.1 = f32[4,8,320,128]{3,2,1,0:T(8,128)} fusion(f32[4,8,128,320]{2,3,1,0:T(8,128)S(1)} %fusion.34, f32[4,8,128,320]{2,3,1,0:T(8,128)S(1)} %fusion.51, bf16[4,1,320,128]{3,2,1,0:T(8,128)(2,1)S(1)} %collective-permute-done.3, bf16[4,8,320,128]{3,2,1,0:T(8,128)(2,1)S(1)} %get-tuple-element.11, bf16[3,3,320,320]{3,2,1,0:T(8,128)(2,1)S(1)} %copy-done.2), kind=kOutput, calls=%fused_computation.34 | convolution fusion | flops 846725120 | bytes 18923520 | tf_op jit(solution)/shard_map/oc,frcw->frow/dot_general | solution.py:30
  83.0 7.3 %fusion.19 = (bf16[4,8,320,128]{3,2,1,0:T(8,128)(2,1)S(1)}, bf16[4,8,320,128]{3,2,1,0:T(8,128)(2,1)}) fusion(f32[4,8,320,127]{3,2,1,0:T(8,128)S(1)} %slice.169, bf16[4,1,320,128]{3,2,1,0:T(8,128)(2,1)} %copy-done.3, bf16[4,8,320,128]{3,2,1,0:T(8,128)(2,1)S(1)} %get-tuple-element.11, bf16[3,3,320,320]{3,2,1,0:T(8,128)(2,1)} %param.9, ...), kind=kOutput, calls=%fused_computation.28 | convolution fusion | flops 862453760 | bytes 31991040 | tf_op jit(solution)/shard_map/oc,frcw->frow/dot_general | solution.py:30
  90.4 5.3 %collective-permute-start.4 = (bf16[1,8,320,128]{3,2,1,0:T(8,128)(2,1)S(1)}, bf16[1,8,320,128]{3,2,1,0:T(8,128)(2,1)S(1)}, u32[]{:S(2)}, u32[]{:S(2)}) collective-permute-start(bf16[1,8,320,128]{3,2,1,0:T(8,128)(2,1)S(1)} %get-tuple-element.6), channel_id=1, source_target_pairs={{0,8},{8,16},{16,24},{24,32},{32,40},{40,48},{48,56},{56,64},{64,7... | collective-permute-start | bytes 1966088 | tf_op jit(solution)/shard_map/ppermute | solution.py:14
  95.7 2.1 %collective-permute-start.5 = (bf16[1,8,320,128]{3,2,1,0:T(8,128)(2,1)S(1)}, bf16[1,8,320,128]{3,2,1,0:T(8,128)(2,1)S(1)}, u32[]{:S(2)}, u32[]{:S(2)}) collective-permute-start(bf16[1,8,320,128]{3,2,1,0:T(8,128)(2,1)S(1)} %get-tuple-element.5), channel_id=1, source_target_pairs={{8,0},{16,8},{24,16},{32,24},{40,32},{48,40},{56,48},{64,56},{72,6... | collective-permute-start | bytes 1966088 | tf_op jit(solution)/shard_map/ppermute | solution.py:15
  99.4 3.8 %collective-permute-done.4 = bf16[1,8,320,128]{3,2,1,0:T(8,128)(2,1)S(1)} collective-permute-done((bf16[1,8,320,128]{3,2,1,0:T(8,128)(2,1)S(1)}, bf16[1,8,320,128]{3,2,1,0:T(8,128)(2,1)S(1)}, u32[]{:S(2)}, u32[]{:S(2)}) %collective-permute-start.4) | collective-permute-done | bytes 655392 | tf_op jit(solution)/shard_map/ppermute | solution.py:14
  104.7 4.1 %collective-permute-done.5 = bf16[1,8,320,128]{3,2,1,0:T(8,128)(2,1)S(1)} collective-permute-done((bf16[1,8,320,128]{3,2,1,0:T(8,128)(2,1)S(1)}, bf16[1,8,320,128]{3,2,1,0:T(8,128)(2,1)S(1)}, u32[]{:S(2)}, u32[]{:S(2)}) %collective-permute-start.5) | collective-permute-done | bytes 655392 | tf_op jit(solution)/shard_map/ppermute | solution.py:15
  108.8 3.0 %fusion.15 = bf16[4,8,320,128]{3,2,1,0:T(8,128)(2,1)} fusion(bf16[4,8,320,128]{3,2,1,0:T(8,128)(2,1)S(1)} %copy-done, f32[4,8,128,320]{2,3,1,0:T(8,128)S(1)} %fusion.39, f32[4,8,128,320]{2,3,1,0:T(8,128)S(1)} %fusion.24, f32[320]{0:T(512)S(1)} %copy-done.6, bf16[1,8,320,128]{3,2,1,0:T(8,128)(2,1)S(1)} %collective-permute-done.5, ...), kind=kOutput, calls=%fused_computation.24 | convolution fusion | flops 851968000 | bytes 19253248 | tf_op jit(solution)/shard_map/oc,frcw->frow/dot_general | solution.py:66
  (33 shorter events, 15.3 us)
Async XLA Ops:
  0.0 11.0 %copy-start.1 = (bf16[3,3,320,320]{3,2,1,0:T(8,128)(2,1)S(1)}, bf16[3,3,320,320]{3,2,1,0:T(8,128)(2,1)}, u32[]{:S(2)}) copy-start(bf16[3,3,320,320]{3,2,1,0:T(8,128)(2,1)} %param.8) | copy-start | bytes 5529604
  3.3 22.5 %collective-permute-start.1 = (bf16[4,1,320,128]{3,2,1,0:T(8,128)(2,1)S(1)}, bf16[4,1,320,128]{3,2,1,0:T(8,128)(2,1)S(1)}, u32[]{:S(2)}, u32[]{:S(2)}) collective-permute-start(bf16[4,1,320,128]{3,2,1,0:T(8,128)(2,1)S(1)} %get-tuple-element.9), channel_id=1, source_target_pairs={{1,0},{2,1},{3,2},{4,3},{5,4},{6,5},{7,6},{9,8},{10,9},{11,10},{12... | collective-permute-start | bytes 983048 | tf_op jit(solution)/shard_map/ppermute | solution.py:15
  5.3 19.0 %collective-permute-start = (bf16[4,1,320,128]{3,2,1,0:T(8,128)(2,1)S(1)}, bf16[4,1,320,128]{3,2,1,0:T(8,128)(2,1)S(1)}, u32[]{:S(2)}, u32[]{:S(2)}) collective-permute-start(bf16[4,1,320,128]{3,2,1,0:T(8,128)(2,1)S(1)} %get-tuple-element.10), channel_id=1, source_target_pairs={{0,1},{1,2},{2,3},{3,4},{4,5},{5,6},{6,7},{8,9},{9,10},{10,11},{11... | collective-permute-start | bytes 983048 | tf_op jit(solution)/shard_map/ppermute | solution.py:14
  25.8 8.0 %copy-start.4 = (bf16[4,1,320,128]{3,2,1,0:T(8,128)(2,1)}, bf16[4,1,320,128]{3,2,1,0:T(8,128)(2,1)S(1)}, u32[]{:S(2)}) copy-start(bf16[4,1,320,128]{3,2,1,0:T(8,128)(2,1)S(1)} %collective-permute-done.1) | copy-start | bytes 983044
  33.8 4.9 %copy-start.7 = (f32[320]{0:T(512)S(1)}, f32[320]{0:T(512)}, u32[]{:S(2)}) copy-start(f32[320]{0:T(512)} %param.11) | copy-start | bytes 3844
  46.1 2.6 %copy-start.2 = (bf16[3,3,320,320]{3,2,1,0:T(8,128)(2,1)S(1)}, bf16[3,3,320,320]{3,2,1,0:T(8,128)(2,1)}, u32[]{:S(2)}) copy-start(bf16[3,3,320,320]{3,2,1,0:T(8,128)(2,1)} %param.9) | copy-start | bytes 5529604
  50.3 22.5 %collective-permute-start.3 = (bf16[4,1,320,128]{3,2,1,0:T(8,128)(2,1)S(1)}, bf16[4,1,320,128]{3,2,1,0:T(8,128)(2,1)S(1)}, u32[]{:S(2)}, u32[]{:S(2)}) collective-permute-start(bf16[4,1,320,128]{3,2,1,0:T(8,128)(2,1)S(1)} %get-tuple-element.7), channel_id=1, source_target_pairs={{1,0},{2,1},{3,2},{4,3},{5,4},{6,5},{7,6},{9,8},{10,9},{11,10},{12... | collective-permute-start | bytes 983048 | tf_op jit(solution)/shard_map/ppermute | solution.py:15
  52.2 19.0 %collective-permute-start.2 = (bf16[4,1,320,128]{3,2,1,0:T(8,128)(2,1)S(1)}, bf16[4,1,320,128]{3,2,1,0:T(8,128)(2,1)S(1)}, u32[]{:S(2)}, u32[]{:S(2)}) collective-permute-start(bf16[4,1,320,128]{3,2,1,0:T(8,128)(2,1)S(1)} %get-tuple-element.8), channel_id=1, source_target_pairs={{0,1},{1,2},{2,3},{3,4},{4,5},{5,6},{6,7},{8,9},{9,10},{10,11},{11... | collective-permute-start | bytes 983048 | tf_op jit(solution)/shard_map/ppermute | solution.py:14
  72.8 6.3 %copy-start.3 = (bf16[4,1,320,128]{3,2,1,0:T(8,128)(2,1)}, bf16[4,1,320,128]{3,2,1,0:T(8,128)(2,1)S(1)}, u32[]{:S(2)}) copy-start(bf16[4,1,320,128]{3,2,1,0:T(8,128)(2,1)S(1)} %collective-permute-done.3) | copy-start | bytes 983044
  79.1 3.9 %copy-start.8 = (f32[320]{0:T(512)S(1)}, f32[320]{0:T(512)}, u32[]{:S(2)}) copy-start(f32[320]{0:T(512)} %param.12) | copy-start | bytes 3844
  90.3 7.5 %copy-start.5 = (bf16[3,320,320]{2,1,0:T(8,128)(2,1)S(1)}, bf16[3,320,320]{2,1,0:T(8,128)(2,1)}, u32[]{:S(2)}) copy-start(bf16[3,320,320]{2,1,0:T(8,128)(2,1)} %param.10) | copy-start | bytes 1843204
  90.4 12.8 %collective-permute-start.4 = (bf16[1,8,320,128]{3,2,1,0:T(8,128)(2,1)S(1)}, bf16[1,8,320,128]{3,2,1,0:T(8,128)(2,1)S(1)}, u32[]{:S(2)}, u32[]{:S(2)}) collective-permute-start(bf16[1,8,320,128]{3,2,1,0:T(8,128)(2,1)S(1)} %get-tuple-element.6), channel_id=1, source_target_pairs={{0,8},{8,16},{16,24},{24,32},{32,40},{40,48},{48,56},{56,64},{64,7... | collective-permute-start | bytes 1966088 | tf_op jit(solution)/shard_map/ppermute | solution.py:14
  95.7 13.1 %collective-permute-start.5 = (bf16[1,8,320,128]{3,2,1,0:T(8,128)(2,1)S(1)}, bf16[1,8,320,128]{3,2,1,0:T(8,128)(2,1)S(1)}, u32[]{:S(2)}, u32[]{:S(2)}) collective-permute-start(bf16[1,8,320,128]{3,2,1,0:T(8,128)(2,1)S(1)} %get-tuple-element.5), channel_id=1, source_target_pairs={{8,0},{16,8},{24,16},{32,24},{40,32},{48,40},{56,48},{64,56},{72,6... | collective-permute-start | bytes 1966088 | tf_op jit(solution)/shard_map/ppermute | solution.py:15
  99.4 9.4 %copy-start = (bf16[4,8,320,128]{3,2,1,0:T(8,128)(2,1)S(1)}, bf16[4,8,320,128]{3,2,1,0:T(8,128)(2,1)}, u32[]{:S(2)}) copy-start(bf16[4,8,320,128]{3,2,1,0:T(8,128)(2,1)} %get-tuple-element.14) | copy-start | bytes 7864324
  99.4 9.4 %copy-start.6 = (f32[320]{0:T(512)S(1)}, f32[320]{0:T(512)}, u32[]{:S(2)}) copy-start(f32[320]{0:T(512)} %param.13) | copy-start | bytes 3844
where the time goes:
time: 112 us
  matrix products  54.1 us (48%)
  waiting for transfers between devices  28.2 us (25%)
  starting transfers between devices  22.8 us (20%)
  other arithmetic  3.25 us (3%)
  local copies, waits for them, and re-layouts  3.05 us (3%)
    dot_general x18, matrix products, conv_rows(): jnp.einsum('oc,frcw->frow', kernel[row_tap, column_tap], activated[:, row...  48.1 us
    ppermute x3, waiting for transfers between devices, padded(): before = lax.ppermute(last, axis, up)  24.2 us
    ppermute x3, starting transfers between devices, padded(): before = lax.ppermute(last, axis, up)  16.8 us
    dot_general x3, matrix products, body(): jnp.einsum('oc,frcw->frow', temporal_mix[frame_tap], activated[frame_tap:...  6.05 us
    ppermute x3, starting transfers between devices, padded(): after = lax.ppermute(first, axis, down)  6.03 us
    ppermute x3, waiting for transfers between devices, padded(): after = lax.ppermute(first, axis, down)  4.07 us
    convert_element_type x1, other arithmetic, silu_round(): return jax.nn.silu(values.astype(jnp.float32)).astype(jnp.bfloat16)  3.25 us
    slice x2, local copies, waits for them, and re-layouts, conv_rows(): shifted_out = jnp.concatenate([partials[2][..., 1:], zero_col], axis=3)  2.83 us
  transfers between devices with their start and end apart: 6, of which 4 were waited for; matrix products, arithmetic and copies ran while one was open for 11% of the time, Pallas kernels for 0%

commit v1 on v0

v1 whole, which is shorter than its diff:
```python
import jax
import jax.numpy as jnp
from jax import lax
from jax.experimental import pallas as pl
from jax.experimental.pallas import tpu as pltpu
from jax.sharding import PartitionSpec as P


BF = jnp.bfloat16
F32 = jnp.float32
VM = pl.BlockSpec(memory_space=pltpu.VMEM)
SM = pl.BlockSpec(memory_space=pltpu.SMEM)
HBM = pl.BlockSpec(memory_space=pltpu.HBM)


def silu(v):
    return v * (0.5 + 0.5 * jnp.tanh(0.5 * v))


def params(mib):
    return pltpu.CompilerParams(vmem_limit_bytes=mib * 2**20)


def fill(S, base, v):
    C, W = v.shape
    a = silu(v).astype(BF)
    lane = lax.broadcasted_iota(jnp.int32, (C, W), 1)
    z = jnp.zeros_like(a)
    S[pl.ds(base, C), :] = jnp.where(lane == 0, z, pltpu.roll(a, 1, 1))
    S[pl.ds(base + C, C), :] = a
    S[pl.ds(base + 2 * C, C), :] = jnp.where(lane == W - 1, z, pltpu.roll(a, W - 1, 1))


def dot_pair(w_ref, S, base, step, depth):
    acc = None
    for k in range(0, depth, 256):
        n = min(256, depth - k)
        rhs = jnp.concatenate([S[pl.ds(base + k, n), :], S[pl.ds(base + step + k, n), :]], axis=1)
        p = jnp.dot(w_ref[:, k:k + n], rhs, preferred_element_type=F32)
        acc = p if acc is None else acc + p
    return acc


class Pipe:
    def __init__(self):
        self.pending = None

    def step(self, dots, post, fills=()):
        outs = dots()
        for f in fills:
            f()
        self.flush()
        self.pending = lambda: post(outs)

    def flush(self):
        if self.pending is not None:
            self.pending()
        self.pending = None


def halves(o):
    return [o[:, :o.shape[1] // 2], o[:, o.shape[1] // 2:]]


def row_side():
    return 1 - lax.axis_index("row") % 2


def odd_clip():
    return lax.axis_index("clip") % 2


def sends_kernel(v, a, b1, b2, sems):
    FR, H = v.shape[:2]
    side = row_side()
    ra, rb = side * (H - 2), (1 - side) * (H - 2)
    copies = [
        (v.at[:, pl.ds(ra, 2)], a),
        (v.at[pl.ds(0, 1), pl.ds(rb, 2)], b1.at[pl.ds(0, 1)]),
        (v.at[pl.ds(FR - 1, 1), pl.ds(rb, 2)], b1.at[pl.ds(1, 1)]),
        (v.at[pl.ds(1, FR - 2), pl.ds(rb, 2)], b2),
    ]
    copies = [pltpu.make_async_copy(x, y, sems.at[n]) for n, (x, y) in enumerate(copies)]
    for c in copies:
        c.start()
    for c in copies:
        c.wait()


def interior_kernel(v, k1, k2, kt, b1, b2, b3, fe, so, w1, w2, wt, bias, S1, S2, F1, m1, m2, mt, sems):
    FR, H, C, W = v.shape
    T = 3 * C
    pipe = Pipe()
    loads = [pltpu.make_async_copy(x, y, sems.at[n]) for n, (x, y) in enumerate(((k1, m1), (k2, m2), (kt, mt)))]
    for c in loads:
        c.start()

    def spread(n, src, dst, taps):
        loads[n].wait()
        for t in range(taps):
            dst[:, t * C:(t + 1) * C] = src[t // 3, t % 3] if taps == 9 else src[t]

    for n, b in enumerate((b1, b2, b3)):
        bias[n] = jnp.broadcast_to(b[...][None, :], (W, C)).T

    def rows_in(g, rows):
        def run():
            for q in range(2):
                for h in rows:
                    fill(S1.at[2 * g + q], h * T, v[2 * g + q, h].astype(F32))

        return run

    for g in range(FR // 2):
        last = g == FR // 2 - 1

        def post_one(p, g=g):
            def run(outs):
                for q in range(2):
                    for e, o in enumerate(halves(outs[q])):
                        h = 2 * p + e + 1
                        f = (v[2 * g + q, h].astype(F32) + bias[0] + o).astype(BF)
                        F1[2 * g + q, h - 1] = f
                        if h in (1, 2):
                            fe[2 * g + q, h - 1] = f
                        if h in (H - 3, H - 2):
                            fe[2 * g + q, h - (H - 3) + 2] = f
                        fill(S2.at[2 * g + q], (h - 1) * T, f.astype(F32))

            return run

        def post_two(p, g=g):
            def run(outs):
                for q in range(2):
                    for e, o in enumerate(halves(outs[q])):
                        h = 2 * p + e
                        so[2 * g + q, h] = (F1[2 * g + q, h + 1].astype(F32) + bias[1] + o).astype(BF)

            return run

        def dots(w, S, p, g=g):
            return lambda: [dot_pair(w, S.at[2 * g + q], 2 * p * T, T, 3 * T) for q in range(2)]

        if g == 0:
            rows_in(0, range(4))()
            spread(0, m1, w1, 9)
        n1, n2 = (H - 2) // 2, (H - 4) // 2
        for p in range(n1):
            more = [rows_in(g, (2 * p + 4, 2 * p + 5))] if 2 * p + 5 < H else []
            if g == 0 and p == 0:
                more.append(lambda: spread(1, m2, w2, 9))
            if g == 0 and p == 1:
                more.append(lambda: spread(2, mt, wt, 3))
            pipe.step(dots(w1, S1, p), post_one(p), more)
        for p in range(n2):
            more = [rows_in(g + 1, (2 * p, 2 * p + 1))] if not last and p < 2 else ()
            pipe.step(dots(w2, S2, p), post_two(p), more)
    pipe.flush()


def edge_kernel(frames, temporal):
    def kernel(v, ha, hb, fe, so, w1, w2, bias, se, *rest):
        H, C = v.shape[1], v.shape[2]
        T = 3 * C
        te, (S1, S2, X, Y) = (rest[:2], rest[2:]) if temporal else ((), rest)
        pipe = Pipe()
        row, rows = lax.axis_index("row"), lax.axis_size("row")
        sa = row_side()
        sides = [sa, 1 - sa]
        inside = [jnp.where(s == 0, row > 0, row < rows - 1) for s in sides]
        gains = [[jnp.where((s == e) & ~ok, 0.0, 1.0).astype(F32) for e in range(2)] for s, ok in zip(sides, inside)]
        N = len(frames)
        at = list(range(N))
        fs = list(frames)
        if temporal:
            odd = odd_clip()
            at = [odd, 1 - odd]
            fs = [frames[0] + a * (frames[1] - frames[0]) for a in at]

        def fills(n):
            f = fs[n]
            for q, s in enumerate(sides):
                b = 2 * n + q
                halo = ha.at[f] if q == 0 else hb.at[at[n]]
                for k in range(2):
                    X[b, 2 * s + k] = halo[k]
                    X[b, 2 - 2 * s + k] = v[f, s * (H - 2) + k]
                for k in range(4):
                    fill(S1.at[b], k * T, X[b, k].astype(F32))

        def dots(w, S, n):
            return lambda: [dot_pair(w, S.at[2 * n + q], 0, T, 3 * T) for q in range(2)]

        def post_one(n):
            def run(outs):
                for q, s in enumerate(sides):
                    b = 2 * n + q
                    for e, o in enumerate(halves(outs[q])):
                        x = (X[b, 1 + e].astype(F32) + bias[0] + o).astype(BF)
                        Y[b, 2 * s + e] = x
                        fill(S2.at[b], pl.multiple_of((2 * s + e) * T, T), x.astype(F32) * gains[q][e])

            return run

        def known(n):
            for q, s in enumerate(sides):
                b = 2 * n + q
                for k in range(2):
                    x = fe[fs[n], 2 * s + k]
                    Y[b, 2 - 2 * s + k] = x
                    fill(S2.at[b], pl.multiple_of((2 - 2 * s + k) * T, T), x.astype(F32))

        def post_two(n):
            def run(outs):
                for q in range(2):
                    for e, o in enumerate(halves(outs[q])):
                        y = (Y[2 * n + q, 1 + e].astype(F32) + bias[1] + o).astype(BF)
                        se[n, 2 * q + e] = y
                        if temporal:
                            te[n][e + q * (H - 2)] = silu(y.astype(F32)).astype(BF)

            return run

        def middle(n):
            if temporal:
                for h in range(H - 4):
                    te[n][h + 2] = silu(so[fs[n], h].astype(F32)).astype(BF)

        fills(0)
        for n in range(N):
            more = [lambda n=n: known(n)]
            if n + 1 < N:
                more.append(lambda n=n: fills(n + 1))
            pipe.step(dots(w1, S1, n), post_one(n), more)
        for n in range(N):
            pipe.step(dots(w2, S2, n), post_two(n), [lambda n=n: middle(n)])
        pipe.flush()

    return kernel


def temporal_kernel(so, sa, sb, own_far, own_near, far, near, wt, bias, out, S, stage, sems):
    FR, HI, C, _ = so.shape
    H = HI + 4
    pipe = Pipe()
    odd = odd_clip()
    slot = {0: (sa, odd), FR - 1: (sa, 1 - odd), 1: (sb, 0), 2: (sb, 1)}

    def second(f, h):
        if 2 <= h < H - 2:
            return so.at[f, h - 2]
        ref, n = slot[f]
        return ref.at[n, h if h < 2 else h - (H - 4)]

    def fills(p):
        for e in range(2):
            h = 2 * p + e
            for f in range(1, FR - 1):
                S[h, pl.ds((f + 1) * C, C), :] = silu(second(f, h)[...].astype(F32)).astype(BF)
            for ref, even_at, odd_at in (
                (far, 0, FR + 1), (own_far, 1, FR), (own_near, FR, 1), (near, FR + 1, 0)
            ):
                to = pl.multiple_of((even_at + odd * (odd_at - even_at)) * C, C)
                S[h, pl.ds(to, C), :] = ref[h]

    side = row_side()

    def copy(p, f):
        to = {0: side * (H - 2), H // 2 - 1: (1 - side) * (H - 2)}.get(p, 2 * p)
        return pltpu.make_async_copy(stage.at[f, pl.ds(2 * p, 2)], out.at[f, pl.ds(to, 2)], sems.at[p, f])

    def dots(p, fs):
        def run():
            outs = []
            for f in fs:
                acc = None
                for k in range(0, 3 * C, 256):
                    n = min(256, 3 * C - k)
                    rhs = jnp.concatenate([S[2 * p + e, pl.ds(f * C + k, n), :] for e in range(2)], axis=1)
                    d = jnp.dot(wt[:, k:k + n], rhs, preferred_element_type=F32)
                    acc = d if acc is None else acc + d
                outs.append(acc)
            return outs

        return run

    def post(p, fs):
        def run(outs):
            for f, o2 in zip(fs, outs):
                for e, o in enumerate(halves(o2)):
                    h = 2 * p + e
                    stage[f, h] = (second(f, h)[...].astype(F32) + bias[2] + o).astype(BF)
                copy(p, f).start()

        return run

    fills(0)
    n = H // 2
    for p in range(n):
        pipe.step(dots(p, (0, 1)), post(p, (0, 1)), [lambda p=p: fills(p + 1)] if p + 1 < n else ())
        pipe.step(dots(p, (2, 3)), post(p, (2, 3)))
    pipe.flush()
    for p in range(n):
        for f in range(FR):
            copy(p, f).wait()


def in_hbm(x):
    return pltpu.with_memory_space_constraint(x, pltpu.HBM)


def shape(*dims, dtype=BF):
    return jax.ShapeDtypeStruct(dims, dtype)


def body(video, spatial_one, spatial_two, temporal_mix, bias_one, bias_two, bias_three):
    FR, H, C, W = video.shape
    T = 3 * C
    rows = lax.axis_size("row")
    swap_a = [(i, i ^ 1) for i in range(rows)]
    swap_b = [p for i in range(1, rows - 1, 2) for p in ((i, i + 1), (i + 1, i))]
    groups = ((0, FR - 1), tuple(range(1, FR - 1)))
    own_a, own_b1, own_b2 = pl.pallas_call(
        sends_kernel,
        in_specs=[HBM],
        out_specs=[VM] * 3,
        out_shape=[shape(FR, 2, C, W), shape(2, 2, C, W), shape(FR - 2, 2, C, W)],
        scratch_shapes=[pltpu.SemaphoreType.DMA((4,))],
        compiler_params=params(8),
        name="sends",
    )(in_hbm(video))
    halo_a = lax.ppermute(own_a, "row", swap_a)
    halo_b1 = lax.ppermute(own_b1, "row", swap_b)
    halo_b2 = lax.ppermute(own_b2, "row", swap_b)
    halos = ((halo_a, halo_b1), (halo_a, halo_b2))
    fe, so, w1, w2, wt, bias = pl.pallas_call(
        interior_kernel,
        in_specs=[VM, HBM, HBM, HBM, VM, VM, VM],
        out_specs=[VM] * 6,
        out_shape=[shape(FR, 4, C, W), shape(FR, H - 4, C, W), shape(C, 9 * C), shape(C, 9 * C), shape(C, 3 * C),
                   shape(3, C, W, dtype=F32)],
        scratch_shapes=[
            pltpu.VMEM((FR, H * T, W), BF),
            pltpu.VMEM((FR, (H - 2) * T, W), BF),
            pltpu.VMEM((FR, H - 2, C, W), BF),
            pltpu.VMEM((3, 3, C, C), BF),
            pltpu.VMEM((3, 3, C, C), BF),
            pltpu.VMEM((3, C, C), BF),
            pltpu.SemaphoreType.DMA((3,)),
        ],
        compiler_params=params(40),
        name="interior",
    )(video, *map(in_hbm, (spatial_one, spatial_two, temporal_mix)), bias_one, bias_two, bias_three)

    def edges(n, temporal):
        g = groups[n]
        outs = [shape(len(g), 4, C, W)] + ([shape(H, C, W)] * 2 if temporal else [])
        return pl.pallas_call(
            edge_kernel(g, temporal),
            in_specs=[VM] * 8,
            out_specs=[VM] * len(outs),
            out_shape=outs,
            scratch_shapes=[pltpu.VMEM((2 * len(g), 4 * T, W), BF)] * 2 + [pltpu.VMEM((2 * len(g), 4, C, W), BF)] * 2,
            compiler_params=params(32),
        )(video, *halos[n], fe, so, w1, w2, bias)

    sa, own_far, own_near = edges(0, True)
    clips = lax.axis_size("clip")
    far = lax.ppermute(own_far, "clip", [p for i in range(1, clips - 1, 2) for p in ((i, i + 1), (i + 1, i))])
    near = lax.ppermute(own_near, "clip", [(i, i ^ 1) for i in range(clips)])
    (sb,) = edges(1, False)
    return pl.pallas_call(
        temporal_kernel,
        in_specs=[VM] * 9,
        out_specs=HBM,
        out_shape=shape(FR, H, C, W),
        scratch_shapes=[
            pltpu.VMEM((H, (FR + 2) * C, W), BF),
            pltpu.VMEM((FR, H, C, W), BF),
            pltpu.SemaphoreType.DMA((H // 2, FR)),
        ],
        compiler_params=params(32),
        name="temporal",
    )(so, sa, sb, own_far, own_near, far, near, wt, bias)


def solution(mesh):
    placed = (P("clip", "row", None, None), P(), P(), P(), P(), P(), P())
    return jax.shard_map(body, mesh=mesh, in_specs=placed, out_specs=P("clip", "row", None, None), check_vma=False)
```

time: 112 us -> 67.7 us (0.60)
  the two profiles are of different devices: /device:TPU:113 before, /device:TPU:4 now
where the time goes in v1:
time: 67.7 us; the launch traced here: 67.5 us
  Pallas kernels  31.1 us (46%)
  waiting for transfers between devices  20.2 us (30%)
  starting transfers between devices  14.6 us (22%)
  local copies, waits for them, and re-layouts  1.37 us (2%)
    ppermute x1, waiting for transfers between devices, body(): halo_b2 = lax.ppermute(own_b2, 'row', swap_b)  15.2 us
    pallas_call x1, Pallas kernels, body(): pl.pallas_call(interior_kernel, in_specs=[VM, HBM, HBM, HBM, VM, VM, VM],...  13.1 us
    pallas_call x2, Pallas kernels, edges(): pl.pallas_call(edge_kernel(g, temporal), in_specs=[VM] * 8, out_specs=[VM...  12.1 us
    ppermute x1, waiting for transfers between devices, body(): halo_a = lax.ppermute(own_a, 'row', swap_a)  5.05 us
    ppermute x1, starting transfers between devices, body(): halo_b2 = lax.ppermute(own_b2, 'row', swap_b)  5.05 us
    pallas_call x1, Pallas kernels, body(): pl.pallas_call(temporal_kernel, in_specs=[VM] * 9, out_specs=HBM, out_sha...  4.42 us
    ppermute x1, starting transfers between devices, body(): near = lax.ppermute(own_near, 'clip', [(i, i ^ 1) for i in range(clips)])  3.32 us
    ppermute x1, starting transfers between devices, body(): halo_a = lax.ppermute(own_a, 'row', swap_a)  3.28 us
  transfers between devices with their start and end apart: 5, of which 2 were waited for; matrix products, arithmetic and copies ran while one was open for 0% of the time, Pallas kernels for 28%

profile of v1, /device:TPU:4, one launch (start us, length us, event | category | flops | bytes accessed | tf_op | source)
XLA Modules:
  0.0 67.5 jit_solution(18188316338964203057)
XLA Ops:
  0.0 0.0 copy-start
  0.0 0.0 copy-start.1
  0.0 1.5 %sends.1 = (bf16[4,2,320,128]{3,2,1,0:T(8,128)(2,1)S(1)}, bf16[2,2,320,128]{3,2,1,0:T(8,128)(2,1)S(1)}, bf16[2,2,320,128]{3,2,1,0:T(8,128)(2,1)S(1)}) custom-call(bf16[4,8,320,128]{3,2,1,0:T(8,128)(2,1)} %v.7), custom_call_target="tpu_custom_call" | custom-call | tf_op jit(solution)/shard_map/sends/pallas_call | solution.py:323
  1.5 3.3 %collective-permute-start = (bf16[4,2,320,128]{3,2,1,0:T(8,128)(2,1)S(1)}, bf16[4,2,320,128]{3,2,1,0:T(8,128)(2,1)S(1)}, u32[]{:S(2)}, u32[]{:S(2)}) collective-permute-start(bf16[4,2,320,128]{3,2,1,0:T(8,128)(2,1)S(1)} %get-tuple-element.18), channel_id=1, source_target_pairs={{0,1},{1,0},{2,3},{3,2},{4,5},{5,4},{6,7},{7,6},{8,9},{9,8},{10,11... | collective-permute-start | bytes 1966088 | tf_op jit(solution)/shard_map/ppermute | solution.py:332
  4.7 2.2 %collective-permute-start.1 = (bf16[2,2,320,128]{3,2,1,0:T(8,128)(2,1)S(1)}, bf16[2,2,320,128]{3,2,1,0:T(8,128)(2,1)S(1)}, u32[]{:S(2)}, u32[]{:S(2)}) collective-permute-start(bf16[2,2,320,128]{3,2,1,0:T(8,128)(2,1)S(1)} %get-tuple-element.19), channel_id=1, source_target_pairs={{1,2},{2,1},{3,4},{4,3},{5,6},{6,5},{9,10},{10,9},{11,12},{12,11},... | collective-permute-start | bytes 983048 | tf_op jit(solution)/shard_map/ppermute | solution.py:333
  7.0 0.0 copy-done
  7.0 0.0 copy-done.1
  7.0 0.0 copy-start.2
  7.0 0.7 copy-done.2
  7.7 0.0 copy-start.3
  7.7 0.7 %copy-done.3 = f32[320]{0:T(512)S(1)} copy-done((f32[320]{0:T(512)S(1)}, f32[320]{0:T(512)}, u32[]{:S(2)}) %copy-start.3) | copy-done | bytes 1304
  8.3 13.1 %interior.1 = (bf16[4,4,320,128]{3,2,1,0:T(8,128)(2,1)S(1)}, bf16[4,4,320,128]{3,2,1,0:T(8,128)(2,1)S(1)}, bf16[320,2880]{1,0:T(8,128)(2,1)S(1)}, bf16[320,2880]...) custom-call(bf16[4,8,320,128]{3,2,1,0:T(8,128)(2,1)S(1)} %copy-done, ...), custom_call_target="tpu_custom_call" | custom-call | tf_op jit(solution)/shard_map/interior/pallas_call | solution.py:336
  21.5 0.0 collective-permute-done.1.hb
  21.5 5.1 %collective-permute-done.ha = bf16[4,2,320,128]{3,2,1,0:T(8,128)(2,1)S(1)} collective-permute-done((bf16[4,2,320,128]{3,2,1,0:T(8,128)(2,1)S(1)}, bf16[4,2,320,128]{3,2,1,0:T(8,128)(2,1)S(1)}, u32[]{:S(2)}, u32[]{:S(2)}) %collective-permute-start) | collective-permute-done | bytes 655392 | tf_op jit(solution)/shard_map/ppermute | solution.py:332
  26.6 6.4 %shard_map.73 = (bf16[2,4,320,128]{3,2,1,0:T(8,128)(2,1)S(1)}, bf16[8,320,128]{2,1,0:T(8,128)(2,1)S(1)}, bf16[8,320,128]{2,1,0:T(8,128)(2,1)S(1)}) custom-call(bf16[4,8,320,128]{3,2,1,0:T(8,128)(2,1)S(1)} %copy-done, bf16[4,2,320,128]{3,2,1,0:T(8,128)(2,1)S(1)} %collective-permute-done.ha, bf16[2,2,320,128]{3,2,1,0:T(8,128)(2,1)S(1)} %collective-permute-done.1.hb, ...), custom_call_target="tpu_custom_call" | custom-call | tf_op jit(solution)/shard_map/pallas_call | solution.py:358
  32.9 0.7 %collective-permute-start.3 = (bf16[8,320,128]{2,1,0:T(8,128)(2,1)S(1)}, bf16[8,320,128]{2,1,0:T(8,128)(2,1)S(1)}, u32[]{:S(2)}, u32[]{:S(2)}) collective-permute-start(bf16[8,320,128]{2,1,0:T(8,128)(2,1)S(1)} %get-tuple-element.26.own_far), channel_id=1, source_target_pairs={{8,16},{16,8},{24,32},{32,24},{40,48},{48,40},{56,64},{64,56},{72,... | collective-permute-start | bytes 1966088 | tf_op jit(solution)/shard_map/ppermute | solution.py:369
  33.6 3.3 %collective-permute-start.4 = (bf16[8,320,128]{2,1,0:T(8,128)(2,1)S(1)}, bf16[8,320,128]{2,1,0:T(8,128)(2,1)S(1)}, u32[]{:S(2)}, u32[]{:S(2)}) collective-permute-start(bf16[8,320,128]{2,1,0:T(8,128)(2,1)S(1)} %get-tuple-element.27.own_near), channel_id=1, source_target_pairs={{0,8},{8,0},{16,24},{24,16},{32,40},{40,32},{48,56},{56,48},{64,72... | collective-permute-start | bytes 1966088 | tf_op jit(solution)/shard_map/ppermute | solution.py:370
  37.0 5.0 %collective-permute-start.2 = (bf16[2,2,320,128]{3,2,1,0:T(8,128)(2,1)S(1)}, bf16[2,2,320,128]{3,2,1,0:T(8,128)(2,1)S(1)}, u32[]{:S(2)}, u32[]{:S(2)}) collective-permute-start(bf16[2,2,320,128]{3,2,1,0:T(8,128)(2,1)S(1)} %get-tuple-element.25), channel_id=1, source_target_pairs={{1,2},{2,1},{3,4},{4,3},{5,6},{6,5},{9,10},{10,9},{11,12},{12,11},... | collective-permute-start | bytes 983048 | tf_op jit(solution)/shard_map/ppermute | solution.py:334
  42.0 15.2 %collective-permute-done.2.hb = bf16[2,2,320,128]{3,2,1,0:T(8,128)(2,1)S(1)} collective-permute-done((bf16[2,2,320,128]{3,2,1,0:T(8,128)(2,1)S(1)}, bf16[2,2,320,128]{3,2,1,0:T(8,128)(2,1)S(1)}, u32[]{:S(2)}, u32[]{:S(2)}) %collective-permute-start.2) | collective-permute-done | bytes 327712 | tf_op jit(solution)/shard_map/ppermute | solution.py:334
  57.2 5.7 %shard_map.74.sb = bf16[2,4,320,128]{3,2,1,0:T(8,128)(2,1)S(1)} custom-call(bf16[4,8,320,128]{3,2,1,0:T(8,128)(2,1)S(1)} %copy-done, bf16[4,2,320,128]{3,2,1,0:T(8,128)(2,1)S(1)} %collective-permute-done.ha, bf16[2,2,320,128]{3,2,1,0:T(8,128)(2,1)S(1)} %collective-permute-done.2.hb, bf16[4,4,320,128]{3,2,1,0:T(8,128)(2,1)S(1)} %get-tuple-element.20.fe, ...), custom_call_target="tpu_custom_call" | custom-call | tf_op jit(solution)/shard_map/pallas_call | solution.py:358
  62.9 0.0 collective-permute-done.3.far
  62.9 0.0 collective-permute-done.4.near
  62.9 4.4 %temporal.1 = bf16[4,8,320,128]{3,2,1,0:T(8,128)(2,1)} custom-call(bf16[4,4,320,128]{3,2,1,0:T(8,128)(2,1)S(1)} %get-tuple-element.17.so, bf16[2,4,320,128]{3,2,1,0:T(8,128)(2,1)S(1)} %get-tuple-element.24.sa, bf16[2,4,320,128]{3,2,1,0:T(8,128)(2,1)S(1)} %shard_map.74.sb, bf16[8,320,128]{2,1,0:T(8,128)(2,1)S(1)} %get-tuple-element.26.own_far, ...), custom_call_target="tpu_custom_call" | custom-call | tf_op jit(solution)/shard_map/temporal/pallas_call | solution.py:372
Async XLA Ops:
  0.0 7.0 %copy-start = (bf16[4,8,320,128]{3,2,1,0:T(8,128)(2,1)S(1)}, bf16[4,8,320,128]{3,2,1,0:T(8,128)(2,1)}, u32[]{:S(2)}) copy-start(bf16[4,8,320,128]{3,2,1,0:T(8,128)(2,1)} %v.7) | copy-start | bytes 7864324
  0.0 7.0 %copy-start.1 = (f32[320]{0:T(512)S(1)}, f32[320]{0:T(512)}, u32[]{:S(2)}) copy-start(f32[320]{0:T(512)} %b1.1) | copy-start | bytes 3844
  1.5 25.1 %collective-permute-start = (bf16[4,2,320,128]{3,2,1,0:T(8,128)(2,1)S(1)}, bf16[4,2,320,128]{3,2,1,0:T(8,128)(2,1)S(1)}, u32[]{:S(2)}, u32[]{:S(2)}) collective-permute-start(bf16[4,2,320,128]{3,2,1,0:T(8,128)(2,1)S(1)} %get-tuple-element.18), channel_id=1, source_target_pairs={{0,1},{1,0},{2,3},{3,2},{4,5},{5,4},{6,7},{7,6},{8,9},{9,8},{10,11... | collective-permute-start | bytes 1966088 | tf_op jit(solution)/shard_map/ppermute | solution.py:332
  4.7 16.7 %collective-permute-start.1 = (bf16[2,2,320,128]{3,2,1,0:T(8,128)(2,1)S(1)}, bf16[2,2,320,128]{3,2,1,0:T(8,128)(2,1)S(1)}, u32[]{:S(2)}, u32[]{:S(2)}) collective-permute-start(bf16[2,2,320,128]{3,2,1,0:T(8,128)(2,1)S(1)} %get-tuple-element.19), channel_id=1, source_target_pairs={{1,2},{2,1},{3,4},{4,3},{5,6},{6,5},{9,10},{10,9},{11,12},{12,11},... | collective-permute-start | bytes 983048 | tf_op jit(solution)/shard_map/ppermute | solution.py:333
  7.0 0.7 %copy-start.2 = (f32[320]{0:T(512)S(1)}, f32[320]{0:T(512)}, u32[]{:S(2)}) copy-start(f32[320]{0:T(512)} %b2.1) | copy-start | bytes 3844
  7.7 0.7 %copy-start.3 = (f32[320]{0:T(512)S(1)}, f32[320]{0:T(512)}, u32[]{:S(2)}) copy-start(f32[320]{0:T(512)} %b3.1) | copy-start | bytes 3844
  32.9 30.0 %collective-permute-start.3 = (bf16[8,320,128]{2,1,0:T(8,128)(2,1)S(1)}, bf16[8,320,128]{2,1,0:T(8,128)(2,1)S(1)}, u32[]{:S(2)}, u32[]{:S(2)}) collective-permute-start(bf16[8,320,128]{2,1,0:T(8,128)(2,1)S(1)} %get-tuple-element.26.own_far), channel_id=1, source_target_pairs={{8,16},{16,8},{24,32},{32,24},{40,48},{48,40},{56,64},{64,56},{72,... | collective-permute-start | bytes 1966088 | tf_op jit(solution)/shard_map/ppermute | solution.py:369
  33.6 29.3 %collective-permute-start.4 = (bf16[8,320,128]{2,1,0:T(8,128)(2,1)S(1)}, bf16[8,320,128]{2,1,0:T(8,128)(2,1)S(1)}, u32[]{:S(2)}, u32[]{:S(2)}) collective-permute-start(bf16[8,320,128]{2,1,0:T(8,128)(2,1)S(1)} %get-tuple-element.27.own_near), channel_id=1, source_target_pairs={{0,8},{8,0},{16,24},{24,16},{32,40},{40,32},{48,56},{56,48},{64,72... | collective-permute-start | bytes 1966088 | tf_op jit(solution)/shard_map/ppermute | solution.py:370
  37.0 20.2 %collective-permute-start.2 = (bf16[2,2,320,128]{3,2,1,0:T(8,128)(2,1)S(1)}, bf16[2,2,320,128]{3,2,1,0:T(8,128)(2,1)S(1)}, u32[]{:S(2)}, u32[]{:S(2)}) collective-permute-start(bf16[2,2,320,128]{3,2,1,0:T(8,128)(2,1)S(1)} %get-tuple-element.25), channel_id=1, source_target_pairs={{1,2},{2,1},{3,4},{4,3},{5,6},{6,5},{9,10},{10,9},{11,12},{12,11},... | collective-permute-start | bytes 983048 | tf_op jit(solution)/shard_map/ppermute | solution.py:334

commit v2 on v1

--- a/solution.py
+++ b/solution.py
@@ -87,21 +87,30 @@
         c.wait()
 
 
-def interior_kernel(v, k1, k2, kt, b1, b2, b3, fe, so, w1, w2, wt, bias, S1, S2, F1, m1, m2, mt, sems):
+def interior_kernel(v, k1, k2, kt, b1, b2, b3, fe, so, w1, w2, wt, bias, S1, S2, F1, m1, m2, mt, c1, c2, c3, sems):
     FR, H, C, W = v.shape
     T = 3 * C
     pipe = Pipe()
-    loads = [pltpu.make_async_copy(x, y, sems.at[n]) for n, (x, y) in enumerate(((k1, m1), (k2, m2), (kt, mt)))]
+    loads = [pltpu.make_async_copy(x, y, sems.at[n]) for n, (x, y) in enumerate(
+        ((b1, c1), (b2, c2), (b3, c3), (k1, m1), (k2, m2), (kt, mt)))]
     for c in loads:
         c.start()
 
-    def spread(n, src, dst, taps):
-        loads[n].wait()
-        for t in range(taps):
-            dst[:, t * C:(t + 1) * C] = src[t // 3, t % 3] if taps == 9 else src[t]
-
-    for n, b in enumerate((b1, b2, b3)):
-        bias[n] = jnp.broadcast_to(b[...][None, :], (W, C)).T
+    def spread(n, src, dst):
+        loads[3 + n].wait()
+        for t in range(9):
+            dst[:, t * C:(t + 1) * C] = src[t // 3, t % 3]
+
+    def spread_temporal():
+        loads[5].wait()
+        for r in range(2):
+            for t in range(3):
+                wt[r, :, t * C:(t + 1) * C] = mt[2 - t if r else t]
+
+    def spread_bias():
+        for n, c in enumerate((c1, c2, c3)):
+            loads[n].wait()
+            bias[n] = jnp.broadcast_to(c[...][None, :], (W, C)).T
 
     def rows_in(g, rows):
         def run():
@@ -143,14 +152,15 @@
 
         if g == 0:
             rows_in(0, range(4))()
-            spread(0, m1, w1, 9)
+            spread_bias()
+            spread(0, m1, w1)
         n1, n2 = (H - 2) // 2, (H - 4) // 2
         for p in range(n1):
             more = [rows_in(g, (2 * p + 4, 2 * p + 5))] if 2 * p + 5 < H else []
             if g == 0 and p == 0:
-                more.append(lambda: spread(1, m2, w2, 9))
+                more.append(lambda: spread(1, m2, w2))
             if g == 0 and p == 1:
-                more.append(lambda: spread(2, mt, wt, 3))
+                more.append(spread_temporal)
             pipe.step(dots(w1, S1, p), post_one(p), more)
         for p in range(n2):
             more = [rows_in(g + 1, (2 * p, 2 * p + 1))] if not last and p < 2 else ()
@@ -239,70 +249,85 @@
     return kernel
 
 
-def temporal_kernel(so, sa, sb, own_far, own_near, far, near, wt, bias, out, S, stage, sems):
-    FR, HI, C, _ = so.shape
-    H = HI + 4
-    pipe = Pipe()
-    odd = odd_clip()
-    slot = {0: (sa, odd), FR - 1: (sa, 1 - odd), 1: (sb, 0), 2: (sb, 1)}
-
-    def second(f, h):
-        if 2 <= h < H - 2:
-            return so.at[f, h - 2]
-        ref, n = slot[f]
-        return ref.at[n, h if h < 2 else h - (H - 4)]
-
-    def fills(p):
-        for e in range(2):
-            h = 2 * p + e
-            for f in range(1, FR - 1):
-                S[h, pl.ds((f + 1) * C, C), :] = silu(second(f, h)[...].astype(F32)).astype(BF)
-            for ref, even_at, odd_at in (
-                (far, 0, FR + 1), (own_far, 1, FR), (own_near, FR, 1), (near, FR + 1, 0)
-            ):
-                to = pl.multiple_of((even_at + odd * (odd_at - even_at)) * C, C)
-                S[h, pl.ds(to, C), :] = ref[h]
-
-    side = row_side()
-
-    def copy(p, f):
-        to = {0: side * (H - 2), H // 2 - 1: (1 - side) * (H - 2)}.get(p, 2 * p)
-        return pltpu.make_async_copy(stage.at[f, pl.ds(2 * p, 2)], out.at[f, pl.ds(to, 2)], sems.at[p, f])
-
-    def dots(p, fs):
-        def run():
-            outs = []
-            for f in fs:
-                acc = None
-                for k in range(0, 3 * C, 256):
-                    n = min(256, 3 * C - k)
-                    rhs = jnp.concatenate([S[2 * p + e, pl.ds(f * C + k, n), :] for e in range(2)], axis=1)
-                    d = jnp.dot(wt[:, k:k + n], rhs, preferred_element_type=F32)
-                    acc = d if acc is None else acc + d
-                outs.append(acc)
-            return outs
-
-        return run
-
-    def post(p, fs):
-        def run(outs):
-            for f, o2 in zip(fs, outs):
-                for e, o in enumerate(halves(o2)):
-                    h = 2 * p + e
-                    stage[f, h] = (second(f, h)[...].astype(F32) + bias[2] + o).astype(BF)
-                copy(p, f).start()
-
-        return run
-
-    fills(0)
-    n = H // 2
-    for p in range(n):
-        pipe.step(dots(p, (0, 1)), post(p, (0, 1)), [lambda p=p: fills(p + 1)] if p + 1 < n else ())
-        pipe.step(dots(p, (2, 3)), post(p, (2, 3)))
-    pipe.flush()
-    for p in range(n):
-        for f in range(FR):
-            copy(p, f).wait()
+def temporal_kernel(outer):
+    def kernel(so, sa, sb, own_far, own_near, *rest):
+        if outer:
+            far, near, act, wt, bias, _, out, stage, sems = rest
+        else:
+            wt, bias, out, act, stage, sems = rest
+        FR, HI, C, _ = so.shape
+        H = HI + 4
+        pipe = Pipe()
+        odd = odd_clip()
+        turn = [odd, 1 - odd]
+        side = row_side()
+        fs = [t * (FR - 1) for t in turn] if outer else [1 + t for t in turn]
+        own = [own_far, own_near]
+
+        def second(u, h):
+            if 2 <= h < H - 2:
+                return so[fs[u], h - 2]
+            e = h if h < 2 else h - (H - 4)
+            return sa[u, e] if outer else sb[turn[u], e]
+
+        def fills(p):
+            for h in (2 * p, 2 * p + 1):
+                for u in range(2):
+                    act[turn[u], h] = silu(second(u, h).astype(F32)).astype(BF)
+
+        def window(u, h):
+            if outer:
+                return [(far, near)[u].at[h], own[u].at[h], act.at[turn[u], h]]
+            return [own[u].at[h], act.at[turn[u], h], act.at[turn[1 - u], h]]
+
+        def column(u, h, k, n):
+            parts = []
+            for t, ref in enumerate(window(u, h)):
+                lo, hi = max(k, t * C), min(k + n, (t + 1) * C)
+                if lo < hi:
+                    parts.append(ref[pl.ds(lo - t * C, hi - lo), :])
+            return parts[0] if len(parts) == 1 else jnp.concatenate(parts, axis=0)
+
+        def copy(p, u):
+            to = {0: side * (H - 2), H // 2 - 1: (1 - side) * (H - 2)}.get(p, 2 * p)
+            return pltpu.make_async_copy(stage.at[u, pl.ds(2 * p, 2)], out.at[fs[u], pl.ds(to, 2)], sems.at[p, u])
+
+        def dots(p):
+            def run():
+                outs = []
+                for u in range(2):
+                    acc = None
+                    for k in range(0, 3 * C, 256):
+                        n = min(256, 3 * C - k)
+                        rhs = jnp.concatenate([column(u, 2 * p + e, k, n) for e in range(2)], axis=1)
+                        d = jnp.dot(wt[turn[u], :, k:k + n], rhs, preferred_element_type=F32)
+                        acc = d if acc is None else acc + d
+                    outs.append(acc)
+                return outs
+
+            return run
+
+        def post(p):
+            def run(outs):
+                for u, o2 in enumerate(outs):
+                    for e, o in enumerate(halves(o2)):
+                        h = 2 * p + e
+                        stage[u, h] = (second(u, h).astype(F32) + bias[2] + o).astype(BF)
+                    copy(p, u).start()
+
+            return run
+
+        n = H // 2
+        if not outer:
+            fills(0)
+        for p in range(n):
+            pipe.step(dots(p), post(p), [lambda p=p: fills(p + 1)] if not outer and p + 1 < n else ())
+        pipe.flush()
+        for p in range(n):
+            for u in range(2):
+                copy(p, u).wait()
+
+    return kernel
 
 
 def in_hbm(x):
@@ -335,9 +360,9 @@
     halos = ((halo_a, halo_b1), (halo_a, halo_b2))
     fe, so, w1, w2, wt, bias = pl.pallas_call(
         interior_kernel,
-        in_specs=[VM, HBM, HBM, HBM, VM, VM, VM],
+        in_specs=[VM] + [HBM] * 6,
         out_specs=[VM] * 6,
-        out_shape=[shape(FR, 4, C, W), shape(FR, H - 4, C, W), shape(C, 9 * C), shape(C, 9 * C), shape(C, 3 * C),
+        out_shape=[shape(FR, 4, C, W), shape(FR, H - 4, C, W), shape(C, 9 * C), shape(C, 9 * C), shape(2, C, 3 * C),
                    shape(3, C, W, dtype=F32)],
         scratch_shapes=[
             pltpu.VMEM((FR, H * T, W), BF),
@@ -346,11 +371,14 @@
             pltpu.VMEM((3, 3, C, C), BF),
             pltpu.VMEM((3, 3, C, C), BF),
             pltpu.VMEM((3, C, C), BF),
-            pltpu.SemaphoreType.DMA((3,)),
+            pltpu.VMEM((C,), F32),
+            pltpu.VMEM((C,), F32),
+            pltpu.VMEM((C,), F32),
+            pltpu.SemaphoreType.DMA((6,)),
         ],
         compiler_params=params(40),
         name="interior",
-    )(video, *map(in_hbm, (spatial_one, spatial_two, temporal_mix)), bias_one, bias_two, bias_three)
+    )(video, *map(in_hbm, (spatial_one, spatial_two, temporal_mix, bias_one, bias_two, bias_three)))
 
     def edges(n, temporal):
         g = groups[n]
@@ -366,22 +394,25 @@
 
     sa, own_far, own_near = edges(0, True)
     clips = lax.axis_size("clip")
+    near = lax.ppermute(own_near, "clip", [(i, i ^ 1) for i in range(clips)])
     far = lax.ppermute(own_far, "clip", [p for i in range(1, clips - 1, 2) for p in ((i, i + 1), (i + 1, i))])
-    near = lax.ppermute(own_near, "clip", [(i, i ^ 1) for i in range(clips)])
     (sb,) = edges(1, False)
-    return pl.pallas_call(
-        temporal_kernel,
-        in_specs=[VM] * 9,
-        out_specs=HBM,
-        out_shape=shape(FR, H, C, W),
-        scratch_shapes=[
-            pltpu.VMEM((H, (FR + 2) * C, W), BF),
-            pltpu.VMEM((FR, H, C, W), BF),
-            pltpu.SemaphoreType.DMA((H // 2, FR)),
-        ],
-        compiler_params=params(32),
-        name="temporal",
-    )(so, sa, sb, own_far, own_near, far, near, wt, bias)
+
+    def temporal(outer, ins, **kw):
+        outs = [pltpu.HBM((FR, H, C, W), BF)] + ([] if outer else [shape(2, H, C, W)])
+        return pl.pallas_call(
+            temporal_kernel(outer),
+            in_specs=[VM] * (len(ins) - outer) + [HBM] * outer,
+            out_specs=[HBM] + [VM] * (len(outs) - 1),
+            out_shape=outs,
+            scratch_shapes=[pltpu.VMEM((2, H, C, W), BF), pltpu.SemaphoreType.DMA((H // 2, 2))],
+            compiler_params=params(24),
+            **kw,
+        )(*ins)
+
+    out, act = temporal(0, (so, sa, sb, own_far, own_near, wt, bias), name="temporal_in")
+    ins = (so, sa, sb, own_far, own_near, far, near, act, wt, bias, in_hbm(out))
+    return temporal(1, ins, name="temporal_out", input_output_aliases={len(ins) - 1: 0})[0]
 
 
 def solution(mesh):

time: 67.7 us -> 68.1 us (level)
  the two profiles are of different devices: /device:TPU:4 before, /device:TPU:2 now
where the time goes in v2:
time: 68.1 us; the launch traced here: 67.9 us
  Pallas kernels  31.5 us (46%)
  waiting for transfers between devices  19.9 us (29%)
  starting transfers between devices  16.3 us (24%)
    ppermute x1, waiting for transfers between devices, body(): halo_b2 = lax.ppermute(own_b2, 'row', swap_b)  15.2 us
    pallas_call x1, Pallas kernels, body(): pl.pallas_call(interior_kernel, in_specs=[VM] + [HBM] * 6, out_specs=[VM]...  13.1 us
    pallas_call x2, Pallas kernels, edges(): pl.pallas_call(edge_kernel(g, temporal), in_specs=[VM] * 8, out_specs=[VM...  12 us
    ppermute x1, starting transfers between devices, body(): halo_b2 = lax.ppermute(own_b2, 'row', swap_b)  5.06 us
    pallas_call x2, Pallas kernels, temporal(): pl.pallas_call(temporal_kernel(outer), in_specs=[VM] * (len(ins) - outer)...  4.91 us
    ppermute x1, waiting for transfers between devices, body(): halo_a = lax.ppermute(own_a, 'row', swap_a)  4.73 us
    ppermute x1, starting transfers between devices, body(): halo_b1 = lax.ppermute(own_b1, 'row', swap_b)  3.91 us
    ppermute x1, starting transfers between devices, body(): near = lax.ppermute(own_near, 'clip', [(i, i ^ 1) for i in range(clips)])  3.32 us
  transfers between devices with their start and end apart: 5, of which 2 were waited for; matrix products, arithmetic and copies ran while one was open for 0% of the time, Pallas kernels for 31%

profile of v2, /device:TPU:2, one launch (start us, length us, event | category | flops | bytes accessed | tf_op | source)
XLA Modules:
  0.0 67.9 jit_solution(6963790025918251500)
XLA Ops:
  0.0 0.0 copy-start
  0.0 1.5 %sends.1 = (bf16[4,2,320,128]{3,2,1,0:T(8,128)(2,1)S(1)}, bf16[2,2,320,128]{3,2,1,0:T(8,128)(2,1)S(1)}, bf16[2,2,320,128]{3,2,1,0:T(8,128)(2,1)S(1)}) custom-call(bf16[4,8,320,128]{3,2,1,0:T(8,128)(2,1)} %v.7), custom_call_target="tpu_custom_call" | custom-call | tf_op jit(solution)/shard_map/sends/pallas_call | solution.py:348
  1.5 3.3 %collective-permute-start = (bf16[4,2,320,128]{3,2,1,0:T(8,128)(2,1)S(1)}, bf16[4,2,320,128]{3,2,1,0:T(8,128)(2,1)S(1)}, u32[]{:S(2)}, u32[]{:S(2)}) collective-permute-start(bf16[4,2,320,128]{3,2,1,0:T(8,128)(2,1)S(1)} %get-tuple-element.20), channel_id=1, source_target_pairs={{0,1},{1,0},{2,3},{3,2},{4,5},{5,4},{6,7},{7,6},{8,9},{9,8},{10,11... | collective-permute-start | bytes 1966088 | tf_op jit(solution)/shard_map/ppermute | solution.py:357
  4.7 3.9 %collective-permute-start.1 = (bf16[2,2,320,128]{3,2,1,0:T(8,128)(2,1)S(1)}, bf16[2,2,320,128]{3,2,1,0:T(8,128)(2,1)S(1)}, u32[]{:S(2)}, u32[]{:S(2)}) collective-permute-start(bf16[2,2,320,128]{3,2,1,0:T(8,128)(2,1)S(1)} %get-tuple-element.21), channel_id=1, source_target_pairs={{1,2},{2,1},{3,4},{4,3},{5,6},{6,5},{9,10},{10,9},{11,12},{12,11},... | collective-permute-start | bytes 983048 | tf_op jit(solution)/shard_map/ppermute | solution.py:358
  8.7 0.0 copy-done
  8.7 13.1 %interior.1 = (bf16[4,4,320,128]{3,2,1,0:T(8,128)(2,1)S(1)}, bf16[4,4,320,128]{3,2,1,0:T(8,128)(2,1)S(1)}, bf16[320,2880]{1,0:T(8,128)(2,1)S(1)}, bf16[320,2880]...) custom-call(bf16[4,8,320,128]{3,2,1,0:T(8,128)(2,1)S(1)} %copy-done, ...), custom_call_target="tpu_custom_call" | custom-call | tf_op jit(solution)/shard_map/interior/pallas_call | solution.py:361
  21.8 0.0 collective-permute-done.1.hb
  21.8 4.7 %collective-permute-done.ha = bf16[4,2,320,128]{3,2,1,0:T(8,128)(2,1)S(1)} collective-permute-done((bf16[4,2,320,128]{3,2,1,0:T(8,128)(2,1)S(1)}, bf16[4,2,320,128]{3,2,1,0:T(8,128)(2,1)S(1)}, u32[]{:S(2)}, u32[]{:S(2)}) %collective-permute-start) | collective-permute-done | bytes 655392 | tf_op jit(solution)/shard_map/ppermute | solution.py:357
  26.5 6.3 %shard_map.73 = (bf16[2,4,320,128]{3,2,1,0:T(8,128)(2,1)S(1)}, bf16[8,320,128]{2,1,0:T(8,128)(2,1)S(1)}, bf16[8,320,128]{2,1,0:T(8,128)(2,1)S(1)}) custom-call(bf16[4,8,320,128]{3,2,1,0:T(8,128)(2,1)S(1)} %copy-done, bf16[4,2,320,128]{3,2,1,0:T(8,128)(2,1)S(1)} %collective-permute-done.ha, bf16[2,2,320,128]{3,2,1,0:T(8,128)(2,1)S(1)} %collective-permute-done.1.hb, ...), custom_call_target="tpu_custom_call" | custom-call | tf_op jit(solution)/shard_map/pallas_call | solution.py:386
  32.9 0.7 %collective-permute-start.3 = (bf16[8,320,128]{2,1,0:T(8,128)(2,1)S(1)}, bf16[8,320,128]{2,1,0:T(8,128)(2,1)S(1)}, u32[]{:S(2)}, u32[]{:S(2)}) collective-permute-start(bf16[8,320,128]{2,1,0:T(8,128)(2,1)S(1)} %get-tuple-element.28.own_far), channel_id=1, source_target_pairs={{8,16},{16,8},{24,32},{32,24},{40,48},{48,40},{56,64},{64,56},{72,... | collective-permute-start | bytes 1966088 | tf_op jit(solution)/shard_map/ppermute | solution.py:398
  33.6 3.3 %collective-permute-start.4 = (bf16[8,320,128]{2,1,0:T(8,128)(2,1)S(1)}, bf16[8,320,128]{2,1,0:T(8,128)(2,1)S(1)}, u32[]{:S(2)}, u32[]{:S(2)}) collective-permute-start(bf16[8,320,128]{2,1,0:T(8,128)(2,1)S(1)} %get-tuple-element.29.own_near), channel_id=1, source_target_pairs={{0,8},{8,0},{16,24},{24,16},{32,40},{40,32},{48,56},{56,48},{64,72... | collective-permute-start | bytes 1966088 | tf_op jit(solution)/shard_map/ppermute | solution.py:397
  36.9 5.1 %collective-permute-start.2 = (bf16[2,2,320,128]{3,2,1,0:T(8,128)(2,1)S(1)}, bf16[2,2,320,128]{3,2,1,0:T(8,128)(2,1)S(1)}, u32[]{:S(2)}, u32[]{:S(2)}) collective-permute-start(bf16[2,2,320,128]{3,2,1,0:T(8,128)(2,1)S(1)} %get-tuple-element.27), channel_id=1, source_target_pairs={{1,2},{2,1},{3,4},{4,3},{5,6},{6,5},{9,10},{10,9},{11,12},{12,11},... | collective-permute-start | bytes 983048 | tf_op jit(solution)/shard_map/ppermute | solution.py:359
  42.0 15.2 %collective-permute-done.2.hb = bf16[2,2,320,128]{3,2,1,0:T(8,128)(2,1)S(1)} collective-permute-done((bf16[2,2,320,128]{3,2,1,0:T(8,128)(2,1)S(1)}, bf16[2,2,320,128]{3,2,1,0:T(8,128)(2,1)S(1)}, u32[]{:S(2)}, u32[]{:S(2)}) %collective-permute-start.2) | collective-permute-done | bytes 327712 | tf_op jit(solution)/shard_map/ppermute | solution.py:359
  57.2 5.7 %shard_map.74.sb = bf16[2,4,320,128]{3,2,1,0:T(8,128)(2,1)S(1)} custom-call(bf16[4,8,320,128]{3,2,1,0:T(8,128)(2,1)S(1)} %copy-done, bf16[4,2,320,128]{3,2,1,0:T(8,128)(2,1)S(1)} %collective-permute-done.ha, bf16[2,2,320,128]{3,2,1,0:T(8,128)(2,1)S(1)} %collective-permute-done.2.hb, bf16[4,4,320,128]{3,2,1,0:T(8,128)(2,1)S(1)} %get-tuple-element.22.fe, ...), custom_call_target="tpu_custom_call" | custom-call | tf_op jit(solution)/shard_map/pallas_call | solution.py:386
  62.8 2.6 %temporal_in.1 = (bf16[4,8,320,128]{3,2,1,0:T(8,128)(2,1)}, bf16[2,8,320,128]{3,2,1,0:T(8,128)(2,1)S(1)}) custom-call(bf16[4,4,320,128]{3,2,1,0:T(8,128)(2,1)S(1)} %get-tuple-element.19.so, bf16[2,4,320,128]{3,2,1,0:T(8,128)(2,1)S(1)} %get-tuple-element.26.sa, bf16[2,4,320,128]{3,2,1,0:T(8,128)(2,1)S(1)} %shard_map.74.sb, ...), custom_call_target="tpu_custom_call" | custom-call | tf_op jit(solution)/shard_map/temporal_in/pallas_call | solution.py:403
  65.4 0.0 collective-permute-done.3.rest_0_
  65.4 0.0 collective-permute-done.4.rest_1_
  65.4 2.3 %temporal_out.1 = bf16[4,8,320,128]{3,2,1,0:T(8,128)(2,1)} custom-call(bf16[4,4,320,128]{3,2,1,0:T(8,128)(2,1)S(1)} %get-tuple-element.19.so, bf16[2,4,320,128]{3,2,1,0:T(8,128)(2,1)S(1)} %get-tuple-element.26.sa, bf16[2,4,320,128]{3,2,1,0:T(8,128)(2,1)S(1)} %shard_map.74.sb, ...), custom_call_target="tpu_custom_call", output_to_operand_aliasing={{}: (10, {})} | custom-call | tf_op jit(solution)/shard_map/temporal_out/pallas_call | solution.py:403
Async XLA Ops:
  0.0 8.7 %copy-start = (bf16[4,8,320,128]{3,2,1,0:T(8,128)(2,1)S(1)}, bf16[4,8,320,128]{3,2,1,0:T(8,128)(2,1)}, u32[]{:S(2)}) copy-start(bf16[4,8,320,128]{3,2,1,0:T(8,128)(2,1)} %v.7) | copy-start | bytes 7864324
  1.5 25.1 %collective-permute-start = (bf16[4,2,320,128]{3,2,1,0:T(8,128)(2,1)S(1)}, bf16[4,2,320,128]{3,2,1,0:T(8,128)(2,1)S(1)}, u32[]{:S(2)}, u32[]{:S(2)}) collective-permute-start(bf16[4,2,320,128]{3,2,1,0:T(8,128)(2,1)S(1)} %get-tuple-element.20), channel_id=1, source_target_pairs={{0,1},{1,0},{2,3},{3,2},{4,5},{5,4},{6,7},{7,6},{8,9},{9,8},{10,11... | collective-permute-start | bytes 1966088 | tf_op jit(solution)/shard_map/ppermute | solution.py:357
  4.7 17.1 %collective-permute-start.1 = (bf16[2,2,320,128]{3,2,1,0:T(8,128)(2,1)S(1)}, bf16[2,2,320,128]{3,2,1,0:T(8,128)(2,1)S(1)}, u32[]{:S(2)}, u32[]{:S(2)}) collective-permute-start(bf16[2,2,320,128]{3,2,1,0:T(8,128)(2,1)S(1)} %get-tuple-element.21), channel_id=1, source_target_pairs={{1,2},{2,1},{3,4},{4,3},{5,6},{6,5},{9,10},{10,9},{11,12},{12,11},... | collective-permute-start | bytes 983048 | tf_op jit(solution)/shard_map/ppermute | solution.py:358
  32.9 32.5 %collective-permute-start.3 = (bf16[8,320,128]{2,1,0:T(8,128)(2,1)S(1)}, bf16[8,320,128]{2,1,0:T(8,128)(2,1)S(1)}, u32[]{:S(2)}, u32[]{:S(2)}) collective-permute-start(bf16[8,320,128]{2,1,0:T(8,128)(2,1)S(1)} %get-tuple-element.28.own_far), channel_id=1, source_target_pairs={{8,16},{16,8},{24,32},{32,24},{40,48},{48,40},{56,64},{64,56},{72,... | collective-permute-start | bytes 1966088 | tf_op jit(solution)/shard_map/ppermute | solution.py:398
  33.6 31.8 %collective-permute-start.4 = (bf16[8,320,128]{2,1,0:T(8,128)(2,1)S(1)}, bf16[8,320,128]{2,1,0:T(8,128)(2,1)S(1)}, u32[]{:S(2)}, u32[]{:S(2)}) collective-permute-start(bf16[8,320,128]{2,1,0:T(8,128)(2,1)S(1)} %get-tuple-element.29.own_near), channel_id=1, source_target_pairs={{0,8},{8,0},{16,24},{24,16},{32,40},{40,32},{48,56},{56,48},{64,72... | collective-permute-start | bytes 1966088 | tf_op jit(solution)/shard_map/ppermute | solution.py:397
  36.9 20.2 %collective-permute-start.2 = (bf16[2,2,320,128]{3,2,1,0:T(8,128)(2,1)S(1)}, bf16[2,2,320,128]{3,2,1,0:T(8,128)(2,1)S(1)}, u32[]{:S(2)}, u32[]{:S(2)}) collective-permute-start(bf16[2,2,320,128]{3,2,1,0:T(8,128)(2,1)S(1)} %get-tuple-element.27), channel_id=1, source_target_pairs={{1,2},{2,1},{3,4},{4,3},{5,6},{6,5},{9,10},{10,9},{11,12},{12,11},... | collective-permute-start | bytes 983048 | tf_op jit(solution)/shard_map/ppermute | solution.py:359
